TPU v7x, 32 devices: a whole 2x2x4 slice. The times are simulated.
32 devices in a mesh: dp: 8 (over y, x, core), tensor: 4 (over z).
Axes of the slice: x: 2, y: 2, z: 4, core: 2. Of those that a mesh axis runs over, the one named last changes fastest.
Arguments:
- inputs: bfloat16 [584, 16, 1024], P('tensor', 'dp'), may hold values from -6 to 6
- valid_mask: int32 [16, 584], P('dp'), may hold values from 0 to 1, as said below
- cotangent: bfloat16 [584, 16, 1024], P('tensor', 'dp'), may hold values from -60 to 60
- ln_gain: bfloat16 [2, 1024], P(None, 'dp'), may hold values from 0.25 to 1.75
- d_bias: bfloat16 [4, 1024], P(None, 'dp'), may hold values from -3 to 3
- w_qkv: bfloat16 [1024, 3, 1024], P('dp', None, 'tensor'), may hold values from -0.1875 to 0.1875
- b_qv: bfloat16 [2, 1024], P(None, 'tensor'), may hold values from -3 to 3
- w_o: bfloat16 [1024, 1024], P('tensor', 'dp'), may hold values from -2 to 2
- w_1: bfloat16 [1024, 4096], P('dp', 'tensor'), may hold values from -0.1875 to 0.1875
- b_1: bfloat16 [4096], P('tensor'), may hold values from -3 to 3
- w_2: bfloat16 [4096, 1024], P('tensor', 'dp'), may hold values from -0.09375 to 0.09375
Outputs:
- block_output: bfloat16 [584, 16, 1024], P('tensor', 'dp')
- grad_inputs: float32 [584, 16, 1024], P('tensor', 'dp')
- grad_ln_gain: float32 [2, 1024], P(None, 'dp')
- grad_d_bias: float32 [4, 1024], P(None, 'dp')
- grad_w_qkv: float32 [1024, 3, 1024], P('dp', None, 'tensor')
- grad_b_qv: float32 [2, 1024], P(None, 'tensor')
- grad_w_o: float32 [1024, 1024], P('tensor', 'dp')
- grad_w_1: float32 [1024, 4096], P('dp', 'tensor')
- grad_b_1: float32 [4096], P('tensor')
- grad_w_2: float32 [4096, 1024], P('tensor', 'dp')
Inputs may be any that keep to these rules, and one draw needn't show every extreme that they name: `valid_mask`: each image has exactly 577 positions marked 1, the others 0.
All inputs are finite; a program needn't handle non-finite values.
Results may differ from a plain program's by a relative error of at most 0.017.
Values may be sent and summed in bfloat16 or wider, within the bound.
A program may use at most 128 MiB of HBM per device.

v0:
```python
import jax
import jax.numpy as jnp
from jax import lax
from jax.sharding import PartitionSpec as P

HD = 64
EPSILON = 1e-06
MASKED = -1e30


def layer_norm(values, gain, shift):
    average = jnp.mean(values, axis=-1, keepdims=True)
    centred = values - average
    variance = jnp.mean(centred * centred, axis=-1, keepdims=True)
    return centred * lax.rsqrt(variance + EPSILON) * gain + shift


def gelu_exact(values):
    return jax.nn.gelu(values, approximate=False)


def gather_layer(ln_gain, d_bias, w_qkv, w_o, w_1, w_2):
    return (
        lax.all_gather(ln_gain, "dp", axis=1, tiled=True),
        lax.all_gather(d_bias, "dp", axis=1, tiled=True),
        lax.all_gather(w_qkv, "dp", axis=0, tiled=True),
        lax.all_gather(w_o, "dp", axis=1, tiled=True),
        lax.all_gather(w_1, "dp", axis=0, tiled=True),
        lax.all_gather(w_2, "dp", axis=1, tiled=True),
    )


def masked_scores(queries, keys_part, valid):
    scores = jnp.einsum(
        "qhd,khd->hqk", queries, keys_part, preferred_element_type=jnp.float32
    ) * HD ** (-0.5)
    return jnp.where(valid[None, None, :] > 0, scores, MASKED)


def attend_forward(bundle):
    packed, valid = bundle
    scores = masked_scores(packed[:, 0], packed[:, 1], valid)
    highest = jnp.max(scores, axis=-1, keepdims=True)
    exponent = jnp.exp(scores - highest)
    denominator = jnp.sum(exponent, axis=-1, keepdims=True)
    attention = (exponent / denominator).astype(jnp.bfloat16)
    mixture = jnp.einsum(
        "hqk,khd->qhd", attention, packed[:, 2], preferred_element_type=jnp.float32
    )
    return (mixture.astype(jnp.bfloat16), (highest + jnp.log(denominator))[..., 0])


def attend_backward(bundle):
    packed, grad_mixture, log_total, valid = bundle
    queries = packed[:, 0]
    keys_part = packed[:, 1]
    values_part = packed[:, 2]
    scores = masked_scores(queries, keys_part, valid)
    attention = jnp.exp(scores - log_total[..., None])
    attention_low = attention.astype(jnp.bfloat16)
    grad_values = jnp.einsum(
        "hqk,qhd->khd", attention_low, grad_mixture, preferred_element_type=jnp.float32
    )
    grad_attention = jnp.einsum(
        "qhd,khd->hqk", grad_mixture, values_part, preferred_element_type=jnp.float32
    )
    inner = jnp.sum(attention * grad_attention, axis=-1, keepdims=True)
    grad_scores = (attention * (grad_attention - inner)).astype(jnp.bfloat16)
    factor = HD ** (-0.5)
    grad_queries = (
        jnp.einsum("hqk,khd->qhd", grad_scores, keys_part, preferred_element_type=jnp.float32)
        * factor
    )
    grad_keys = (
        jnp.einsum("hqk,qhd->khd", grad_scores, queries, preferred_element_type=jnp.float32)
        * factor
    )
    return jnp.stack([grad_queries, grad_keys, grad_values], axis=1)


def body(inputs, valid_mask, cotangent, ln_gain, d_bias, w_qkv, b_qv, w_o, w_1, b_1, w_2):
    local_rows, images, model_width = inputs.shape
    layer = gather_layer(ln_gain, d_bias, w_qkv, w_o, w_1, w_2)
    gains = layer[0].astype(jnp.float32)
    shifts = layer[1].astype(jnp.float32)
    wide_qkv = layer[2].reshape(model_width, -1)
    wide_out = layer[3]
    wide_up = layer[4]
    wide_down = layer[5]
    residual = inputs.astype(jnp.float32)
    normed1 = layer_norm(residual, gains[0], shifts[0]).astype(jnp.bfloat16)
    gathered1 = lax.all_gather(normed1, "tensor", axis=0, tiled=True)
    full_length = gathered1.shape[0]
    columns = b_qv.shape[1]
    heads_local = columns // HD
    projected = jnp.dot(gathered1, wide_qkv, preferred_element_type=jnp.float32).reshape(
        full_length, images, 3, columns
    )
    qkv_bias = jnp.stack([b_qv[0], jnp.zeros_like(b_qv[0]), b_qv[1]]).astype(jnp.float32)
    projected_low = (projected + qkv_bias).astype(jnp.bfloat16)
    per_image = jnp.transpose(projected_low, (1, 0, 2, 3)).reshape(
        images, full_length, 3, heads_local, HD
    )
    mixture, log_total = lax.map(attend_forward, (per_image, valid_mask))
    mixture_seq = jnp.transpose(mixture, (1, 0, 2, 3)).reshape(full_length, images, columns)
    segment = mixture_seq
    attn_sum = lax.psum_scatter(
        jnp.dot(segment, wide_out, preferred_element_type=jnp.float32),
        "tensor",
        scatter_dimension=0,
        tiled=True,
    )
    hidden1 = residual + attn_sum + shifts[2]
    normed2 = layer_norm(hidden1, gains[1], shifts[1]).astype(jnp.bfloat16)
    gathered2 = lax.all_gather(normed2, "tensor", axis=0, tiled=True)
    hidden_in = jnp.dot(gathered2, wide_up, preferred_element_type=jnp.float32) + b_1.astype(
        jnp.float32
    )
    active = gelu_exact(hidden_in).astype(jnp.bfloat16)
    segment = active
    branch_sum = lax.psum_scatter(
        jnp.dot(segment, wide_down, preferred_element_type=jnp.float32).astype(jnp.bfloat16),
        "tensor",
        scatter_dimension=0,
        tiled=True,
    ).astype(jnp.float32)
    block_output = (hidden1 + branch_sum + shifts[3]).astype(jnp.bfloat16)
    layer = gather_layer(ln_gain, d_bias, w_qkv, w_o, w_1, w_2)
    wide_qkv = layer[2].reshape(model_width, -1)
    wide_out = layer[3]
    wide_up = layer[4]
    wide_down = layer[5]
    grad_out = cotangent.astype(jnp.float32)
    grad_gathered = lax.all_gather(cotangent, "tensor", axis=0, tiled=True)
    grad_w_2 = jnp.einsum("sif,sid->fd", active, grad_gathered, preferred_element_type=jnp.float32)
    grad_active = jnp.einsum(
        "sid,fd->sif", grad_gathered, wide_down, preferred_element_type=jnp.float32
    )
    grad_hidden_in = jax.vjp(gelu_exact, hidden_in)[1](grad_active)[0]
    grad_b_1 = jnp.sum(grad_hidden_in, axis=(0, 1))
    grad_hidden_low = grad_hidden_in.astype(jnp.bfloat16)
    grad_w_1 = jnp.einsum(
        "sid,sif->df", gathered2, grad_hidden_low, preferred_element_type=jnp.float32
    )
    segment = grad_hidden_low
    grad_normed2 = lax.psum_scatter(
        jnp.einsum("sif,df->sid", segment, wide_up, preferred_element_type=jnp.float32),
        "tensor",
        scatter_dimension=0,
        tiled=True,
    )
    second_pull = jax.vjp(layer_norm, hidden1, gains[1], shifts[1])[1]
    grad_from_norm, gain2_grad, shift2_grad = second_pull(grad_normed2)
    grad_hidden1 = grad_out + grad_from_norm
    grad_attn_low = grad_hidden1.astype(jnp.bfloat16)
    grad_attn_all = lax.all_gather(grad_attn_low, "tensor", axis=0, tiled=True)
    grad_w_o = jnp.einsum(
        "sic,sid->cd", mixture_seq, grad_attn_all, preferred_element_type=jnp.float32
    )
    grad_mixture = jnp.einsum(
        "sid,cd->sic", grad_attn_all, wide_out, preferred_element_type=jnp.float32
    ).astype(jnp.bfloat16)
    grad_mixture_img = jnp.transpose(
        grad_mixture.reshape(full_length, images, heads_local, HD), (1, 0, 2, 3)
    )
    grad_packed = lax.map(attend_backward, (per_image, grad_mixture_img, log_total, valid_mask))
    grad_projected = jnp.transpose(grad_packed, (1, 0, 2, 3, 4)).reshape(
        full_length, images, 3, columns
    )
    grad_b_qv = jnp.stack(
        [
            jnp.sum(grad_projected[:, :, 0], axis=(0, 1)),
            jnp.sum(grad_projected[:, :, 2], axis=(0, 1)),
        ]
    )
    grad_projected_low = grad_projected.reshape(full_length, images, 3 * columns).astype(
        jnp.bfloat16
    )
    grad_w_qkv = jnp.einsum(
        "sid,sic->dc", gathered1, grad_projected_low, preferred_element_type=jnp.float32
    ).reshape(model_width, 3, columns)
    segment = grad_projected_low
    grad_normed1 = lax.psum_scatter(
        jnp.einsum("sic,dc->sid", segment, wide_qkv, preferred_element_type=jnp.float32).astype(
            jnp.bfloat16
        ),
        "tensor",
        scatter_dimension=0,
        tiled=True,
    ).astype(jnp.float32)
    first_pull = jax.vjp(layer_norm, residual, gains[0], shifts[0])[1]
    grad_from_front, gain1_grad, shift1_grad = first_pull(grad_normed1)
    grad_inputs = grad_hidden1 + grad_from_front
    gain_terms = jnp.stack([gain1_grad, gain2_grad])
    shift_terms = jnp.stack(
        [
            shift1_grad,
            shift2_grad,
            jnp.sum(grad_hidden1, axis=(0, 1)),
            jnp.sum(grad_out, axis=(0, 1)),
        ]
    )
    scattered = (
        lax.psum_scatter(
            gain_terms.astype(jnp.bfloat16), "dp", scatter_dimension=1, tiled=True
        ).astype(jnp.float32),
        lax.psum_scatter(
            shift_terms.astype(jnp.bfloat16), "dp", scatter_dimension=1, tiled=True
        ).astype(jnp.float32),
        lax.psum_scatter(
            grad_w_qkv.astype(jnp.bfloat16), "dp", scatter_dimension=0, tiled=True
        ).astype(jnp.float32),
        lax.psum_scatter(
            grad_w_o.astype(jnp.bfloat16), "dp", scatter_dimension=1, tiled=True
        ).astype(jnp.float32),
        lax.psum_scatter(
            grad_w_1.astype(jnp.bfloat16), "dp", scatter_dimension=0, tiled=True
        ).astype(jnp.float32),
        lax.psum_scatter(
            grad_w_2.astype(jnp.bfloat16), "dp", scatter_dimension=1, tiled=True
        ).astype(jnp.float32),
    )
    gain_sum, shift_sum = lax.psum((scattered[0], scattered[1]), "tensor")
    bias_qv_sum, bias_up_sum = lax.psum((grad_b_qv, grad_b_1), "dp")
    return (
        block_output,
        grad_inputs,
        gain_sum,
        shift_sum,
        scattered[2],
        bias_qv_sum,
        scattered[3],
        scattered[4],
        bias_up_sum,
        scattered[5],
    )


def solution(mesh):
    in_specs = (
        P("tensor", "dp", None),
        P("dp", None),
        P("tensor", "dp", None),
        P(None, "dp"),
        P(None, "dp"),
        P("dp", None, "tensor"),
        P(None, "tensor"),
        P("tensor", "dp"),
        P("dp", "tensor"),
        P("tensor"),
        P("tensor", "dp"),
    )
    out_specs = (
        P("tensor", "dp", None),
        P("tensor", "dp", None),
        P(None, "dp"),
        P(None, "dp"),
        P("dp", None, "tensor"),
        P(None, "tensor"),
        P("tensor", "dp"),
        P("dp", "tensor"),
        P("tensor"),
        P("tensor", "dp"),
    )
    return jax.shard_map(body, mesh=mesh, in_specs=in_specs, out_specs=out_specs, check_vma=False)
```

profile of v0, /device:TPU:0, one launch (start us, length us, event | category | flops | bytes accessed | tf_op | source)
XLA Modules:
  0.0 1150.8 jit_solution(2378708454313699446)
XLA Ops:
  10.7 2.0 fusion.80
  13.0 10.4 all_gather.34
  23.4 8.8 all_gather.35
  32.8 2.9 add_convert_fusion.3
  35.8 10.5 all_gather.38
  46.4 45.4 %all-gather.8.cloned.1.call-done = bf16[584,2,1024]{2,1,0:T(2,128)(2,1)} async-done(((bf16[146,2,1024]{2,1,0:T(2,128)(2,1)}), bf16[584,2,1024]{2,1,0:T(2,128)(2,1)}) %all-gather.8.cloned.1.call-update) | async-done | bytes 2392080 | tf_op jit(solution)/shard_map/all_gather | solution.py:92
  91.8 5.7 fusion.58
  97.4 2.8 copy.121
  100.2 11.2 while.22
  108.8 1.8 fusion.130
  111.5 2.0 fusion.89
  113.5 5.9 copy.123
  120.0 13.1 %all-gather.12.cloned.1.call-start = ((), (), s32[]{:S(2)}) async-start(), calls=%async_computation.8 | async-start | bytes 2990080 | tf_op jit(solution)/shard_map/all_gather | solution.py:115
  134.3 158.0 %all-reduce.11.cloned.1.call-done = f32[584,2,1024]{2,1,0:T(2,128)} async-done(((f32[584,2,1024]{2,1,0:T(2,128)}), f32[584,2,1024]{2,1,0:T(2,128)}) %all-reduce.11.cloned.1.call-update) | async-done | bytes 4784144
  292.3 2.3 fusion.99
  298.8 22.0 %all-gather.14.cloned.1.call-done = bf16[1024,1024]{1,0:T(8,128)(2,1)} async-done(((bf16[128,1024]{1,0:T(8,128)(2,1)}), bf16[1024,1024]{1,0:T(8,128)(2,1)}) %all-gather.14.cloned.1.call-update) | async-done | bytes 2097168 | tf_op jit(solution)/shard_map/all_gather | solution.py:28
  320.8 52.6 %all-gather.12.cloned.1.call-done = bf16[584,2,1024]{2,1,0:T(2,128)(2,1)} async-done(((bf16[146,2,1024]{2,1,0:T(2,128)(2,1)}), bf16[584,2,1024]{2,1,0:T(2,128)(2,1)}) %all-gather.12.cloned.1.call-update) | async-done | bytes 2392080 | tf_op jit(solution)/shard_map/all_gather | solution.py:115
  373.4 6.5 fusion.87
  380.0 2.2 copy-done.8
  382.1 12.1 %multiply_convert_fusion.1 = (bf16[584,2,1024]{2,0,1:T(8,128)(2,1)}, f32[584,2,1024]{2,0,1:T(8,128)}) fusion(f32[584,2,1024]{2,0,1:T(8,128)S(1)} %get-tuple-element.161, f32[1024]{0:T(1024)S(1)} %convert_element_type.124, u8[584,1024]{1,0:T(8,128)(4,1)S(1)} %get-tuple-element.107, u8[584,1024]{1,0:T(8,128)(4,1)S(1)} %get-tuple-element.106), kind=kLoop, calls=%fused_computation.55 | loop fusion | flops 84918272 | bytes 13160448 | tf_op jit(solution)/shard_map/convert_element_type | solution.py:119
  394.2 29.9 %all-gather.18.cloned.1.call-done = bf16[584,2,1024]{2,1,0:T(2,128)(2,1)} async-done(((bf16[146,2,1024]{2,1,0:T(2,128)(2,1)}), bf16[584,2,1024]{2,1,0:T(2,128)(2,1)}) %all-gather.18.cloned.1.call-update) | async-done | bytes 2392080 | tf_op jit(solution)/shard_map/all_gather | solution.py:134
  424.2 28.7 %all-gather.16.cloned.1.call-done = bf16[1024,1024]{1,0:T(8,128)(2,1)} async-done(((bf16[1024,128]{1,0:T(8,128)(2,1)}), bf16[1024,1024]{1,0:T(8,128)(2,1)}) %all-gather.16.cloned.1.call-update) | async-done | bytes 2097168 | tf_op jit(solution)/shard_map/all_gather | solution.py:29
  452.9 9.5 fusion.104
  462.5 2.7 fusion.52
  465.2 5.9 copy.131
  471.1 174.2 %all-reduce.13.cloned.1.call-done = f32[584,2,1024]{2,1,0:T(2,128)} async-done(((f32[584,2,1024]{2,1,0:T(2,128)}), f32[584,2,1024]{2,1,0:T(2,128)}) %all-reduce.13.cloned.1.call-update) | async-done | bytes 4784144
  645.3 3.9 multiply_reduce_fusion.1
  649.5 3.1 fusion.98
  653.6 1.8 fusion.94
  655.5 6.8 bitcast_convert_fusion
  662.3 4.0 copy.172
  666.3 7.1 bitcast_convert_fusion.1
  673.7 31.5 %all-gather.20.cloned.1.call-done = bf16[584,2,1024]{2,1,0:T(2,128)(2,1)} async-done(((bf16[146,2,1024]{2,1,0:T(2,128)(2,1)}), bf16[584,2,1024]{2,1,0:T(2,128)(2,1)}) %all-gather.20.cloned.1.call-update) | async-done | bytes 2392080 | tf_op jit(solution)/shard_map/all_gather | solution.py:156
  705.2 3.7 fusion.72
  708.8 2.1 copy.170
  710.9 3.7 fusion.69
  714.6 2.2 copy.137
  716.7 22.0 %while.23 = (s32[]{:T(128)}, f32[2,584,3,4,64]{1,4,3,2,0:T(8,128)}, bf16[2,584,3,4,64]{1,4,3,2,0:T(8,128)(2,1)S(1)}, s32[2,584]{1,0:T(2,128)S(1)}, f32[2,4,584]{...) while((s32[]{:T(128)}, f32[2,584,3,4,64]{1,4,3,2,0:T(8,128)}, ...), condition=%wide.region_15.16_spmd, body=%wide.region_13.15_spmd.sunk | while | flops 894760960 | bytes 83480296 | solution.py:166
  719.5 2.0 multiply_reduce_fusion.5
  721.6 1.9 multiply_convert_fusion.3
  725.8 1.9 copy-done.2
  730.5 2.0 multiply_reduce_fusion.5
  732.5 1.9 multiply_convert_fusion.3
  736.8 1.9 copy-done.2
  738.8 2.5 bitcast_convert_fusion.2
  741.6 4.0 bitcast_convert_fusion.3
  745.9 5.0 fusion.55
  750.9 4.0 copy.129
  754.9 2.1 convolution_convert_fusion
  757.0 4.0 copy.140
  764.6 27.9 %reduce-scatter.17.cloned.1.call-done = bf16[128,1024]{1,0:T(8,128)(2,1)} async-done(((bf16[1024,1024]{1,0:T(8,128)(2,1)}), bf16[128,1024]{1,0:T(8,128)(2,1)}) %reduce-scatter.17.cloned.1.call-update) | async-done | bytes 262160 | tf_op jit(solution)/shard_map/reduce_scatter | solution.py:216
  792.5 1.8 convert_element_type.144
  794.4 1.9 slice_reduce_fusion.1
  796.3 13.8 %all-reduce.4 = (f32[2,256]{1,0:T(2,128)}, f32[1024]{0:T(1024)}) all-reduce(f32[2,256]{1,0:T(2,128)S(1)} %pad_maximum_fusion.2, f32[1024]{0:T(1024)S(1)} %get-tuple-element.162), channel_id=1, replica_groups=mesh['dp'=8,'tensor'=4] {'dp'}, use_global_device_ids=true, to_apply=%region_32.33 | all-reduce | flops 1536 | bytes 12288 | tf_op jit(solution)/shard_map/psum | solution.py:224
  810.1 19.5 %reduce-scatter.23.cloned.1.call-done = bf16[128,256]{1,0:T(8,128)(2,1)} async-done(((bf16[1024,256]{1,0:T(8,128)(2,1)}), bf16[128,256]{1,0:T(8,128)(2,1)}) %reduce-scatter.23.cloned.1.call-update) | async-done | bytes 65552
  831.3 40.0 %reduce-scatter.15.cloned.1.call-done = bf16[128,3,256]{2,0,1:T(8,128)(2,1)} async-done(((bf16[1024,3,256]{2,0,1:T(8,128)(2,1)}), bf16[128,3,256]{2,0,1:T(8,128)(2,1)}) %reduce-scatter.15.cloned.1.call-update) | async-done | bytes 196624 | tf_op jit(solution)/shard_map/reduce_scatter | solution.py:210
  873.0 174.7 %all-reduce.15.cloned.1.call-done = (bf16[584,2,1024]{2,1,0:T(2,128)(2,1)}, bf16[584,2,1024]{2,1,0:T(2,128)(2,1)}) async-done(((bf16[584,2,1024]{2,1,0:T(2,128)(2,1)}, bf16[584,2,1024]{2,1,0:T(2,128)(2,1)}), (bf16[584,2,1024]{2,1,0:T(2,128)(2,1)}, bf16[584,2,1024]{2,1,0:T(2,128)(2,1)})) %all-reduce.15.cloned.1.call-update) | async-done | bytes 4784144
  1049.3 2.3 fusion.85
  1051.9 4.2 fusion.81
  1056.1 4.5 add_add_fusion.2
  1062.5 2.5 add_convert_fusion.1
  1065.0 29.3 %reduce-scatter.19.cloned.1.call-done = bf16[128,2]{1,0:T(8,128)(2,1)} async-done(((bf16[1024,2]{1,0:T(8,128)(2,1)}), bf16[128,2]{1,0:T(8,128)(2,1)}) %reduce-scatter.19.cloned.1.call-update) | async-done | bytes 528
  1095.1 35.8 %reduce-scatter.21.cloned.1.call-done = bf16[128,4]{1,0:T(8,128)(2,1)} async-done(((bf16[1024,4]{1,0:T(8,128)(2,1)}), bf16[128,4]{1,0:T(8,128)(2,1)}) %reduce-scatter.21.cloned.1.call-update) | async-done | bytes 1040
  1131.8 12.3 %all-reduce.5 = (f32[2,128]{1,0:T(2,128)}, f32[4,128]{1,0:T(4,128)}) all-reduce(bf16[2,128]{1,0:T(2,128)(2,1)S(1)} %copy.167, bf16[4,128]{1,0:T(4,128)(2,1)S(1)} %copy.169), channel_id=1, replica_groups=mesh['dp'=8,'tensor'=4] {'tensor'}, use_global_device_ids=true, to_apply=%region_22.23 | all-reduce | flops 768 | bytes 4608 | tf_op jit(solution)/shard_map/psum | solution.py:223
  (175 shorter events, 43.9 us)
Async XLA Ops:
  7.2 28.6 %copy-start.18 = (bf16[256,128]{1,0:T(8,128)(2,1)S(1)}, bf16[256,128]{1,0:T(8,128)(2,1)}, u32[]{:S(2)}) copy-start(bf16[256,128]{1,0:T(8,128)(2,1)} %param.22) | copy-start | bytes 196612
  7.2 39.1 %copy-start.22 = (bf16[2,256]{1,0:T(2,128)(2,1)S(1)}, bf16[2,256]{1,0:T(2,128)(2,1)}, u32[]{:S(2)}) copy-start(bf16[2,256]{1,0:T(2,128)(2,1)} %param.21) | copy-start | bytes 3076
  7.2 39.2 %all-gather.10.cloned.1.call-start = ((), (), s32[]{:S(2)}) async-start(), calls=%async_computation.7 | async-start | bytes 1769472 | tf_op jit(solution)/shard_map/all_gather | solution.py:26
  9.0 82.7 %all-gather.8.cloned.1.call-start = ((), (), s32[]{:S(2)}) async-start(), calls=%async_computation.6 | async-start | bytes 2990080 | tf_op jit(solution)/shard_map/all_gather | solution.py:92
  10.7 86.8 %copy-start.9 = (f32[146,2]{1,0:T(8,128)}, f32[146,2]{1,0:T(8,128)S(1)}, u32[]{:S(2)}) copy-start(f32[146,2]{1,0:T(8,128)S(1)} %broadcast_multiply_fusion.1) | copy-start | bytes 3508
  12.8 10.5 copy-start.19
  13.0 84.5 %copy-start.11 = (f32[146,2]{1,0:T(8,128)}, f32[146,2]{1,0:T(8,128)S(1)}, u32[]{:S(2)}) copy-start(f32[146,2]{1,0:T(8,128)S(1)} %copy.118) | copy-start | bytes 3508
  32.1 65.3 %copy-start.16 = (f32[1,1024]{1,0:T(1,128)}, f32[1,1024]{1,0:T(1,128)S(1)}, u32[]{:S(2)}) copy-start(f32[1,1024]{1,0:T(1,128)S(1)} %get-tuple-element.158) | copy-start | bytes 12292
  35.7 256.6 %all-reduce.11.cloned.1.call-start = ((), (), s32[]{:S(2)}) async-start(), calls=%async_computation.19 | async-start | bytes 9568256
  97.4 2.8 copy-start.15
  101.8 1.4 copy-start.13
  105.0 0.9 copy-start.14
  107.4 1.4 copy-start.13
  110.6 0.9 copy-start.14
  119.4 13.7 %copy-start.27 = (u32[32]{0:T(128)S(1)}, u32[32]{0:T(128)}, u32[]{:S(2)}) copy-start(u32[32]{0:T(128)} %constant.134) | copy-start | bytes 388
  119.4 201.4 %all-gather.14.cloned.1.call-start = ((), (), s32[]{:S(2)}) async-start(), calls=%async_computation.9 | async-start | bytes 2359296 | tf_op jit(solution)/shard_map/all_gather | solution.py:28
  120.0 253.5 %all-gather.12.cloned.1.call-start = ((), (), s32[]{:S(2)}) async-start(), calls=%async_computation.8 | async-start | bytes 2990080 | tf_op jit(solution)/shard_map/all_gather | solution.py:115
  294.6 4.1 copy-start.23
  297.4 126.8 %all-gather.18.cloned.1.call-start = ((), (), s32[]{:S(2)}) async-start(), calls=%async_computation.11 | async-start | bytes 2990080 | tf_op jit(solution)/shard_map/all_gather | solution.py:134
  298.0 154.9 %all-gather.16.cloned.1.call-start = ((), (), s32[]{:S(2)}) async-start(), calls=%async_computation.10 | async-start | bytes 2359296 | tf_op jit(solution)/shard_map/all_gather | solution.py:29
  298.7 346.6 %all-reduce.13.cloned.1.call-start = ((), (), s32[]{:S(2)}) async-start(), calls=%async_computation.20 | async-start | bytes 9568256
  380.0 2.2 copy-start.8
  452.9 9.6 copy-start.25
  462.4 2.7 copy-start.28
  471.1 234.1 %all-gather.20.cloned.1.call-start = ((), (), s32[]{:S(2)}) async-start(), calls=%async_computation.12 | async-start | bytes 2990080 | tf_op jit(solution)/shard_map/all_gather | solution.py:156
  649.4 4.2 copy-start.5
  652.6 1.0 copy-start.3
  655.5 107.1 %reduce-scatter.25.cloned.1.call-start = ((), (), s32[]{:S(2)}) async-start(), calls=%async_computation.18 | async-start | bytes 2359296
  666.3 126.3 %reduce-scatter.17.cloned.1.call-start = ((), (), s32[]{:S(2)}) async-start(), calls=%async_computation.14 | async-start | bytes 2359296 | tf_op jit(solution)/shard_map/reduce_scatter | solution.py:216
  673.4 156.2 %reduce-scatter.23.cloned.1.call-start = ((), (), s32[]{:S(2)}) async-start(), calls=%async_computation.17 | async-start | bytes 589824
  716.9 1.2 copy-start.7
  723.5 2.1 copy-start.1
  725.8 1.9 copy-start.2
  727.8 1.2 copy-start.7
  734.5 2.2 copy-start.1
  736.8 1.9 copy-start.2
  738.7 132.6 %reduce-scatter.15.cloned.1.call-start = ((), (), s32[]{:S(2)}) async-start(), calls=%async_computation.13 | async-start | bytes 1769472 | tf_op jit(solution)/shard_map/reduce_scatter | solution.py:210
  738.8 2.9 copy-start.24
  745.6 302.1 %all-reduce.15.cloned.1.call-start = ((), (), s32[]{:S(2)}) async-start(), calls=%async_computation.21 | async-start | bytes 9568256
  750.9 4.0 copy-start.26
  760.9 1.1 copy-start.6
  761.0 333.4 %reduce-scatter.19.cloned.1.call-start = ((), (), s32[]{:S(2)}) async-start(), calls=%async_computation.15 | async-start | bytes 294912
  763.8 285.6 %copy-start = (bf16[146,2,1024]{2,1,0:T(2,128)(2,1)S(1)}, bf16[146,2,1024]{2,1,0:T(2,128)(2,1)}, u32[]{:S(2)}) copy-start(bf16[146,2,1024]{2,1,0:T(2,128)(2,1)} %param.15) | copy-start | bytes 1794052
  763.8 285.5 %copy-start.10 = (f32[146,2]{1,0:T(8,128)S(1)}, f32[146,2]{1,0:T(8,128)}, u32[]{:S(2)}) copy-start(f32[146,2]{1,0:T(8,128)} %copy-done.9) | copy-start | bytes 3508
  763.8 285.5 %copy-start.17 = (f32[1,1024]{1,0:T(1,128)S(1)}, f32[1,1024]{1,0:T(1,128)}, u32[]{:S(2)}) copy-start(f32[1,1024]{1,0:T(1,128)} %copy-done.16) | copy-start | bytes 12292
  794.3 257.4 %copy-start.20 = (f32[146,2]{0,1:T(2,128)S(1)}, f32[146,2]{0,1:T(2,128)}, u32[]{:S(2)}) copy-start(f32[146,2]{0,1:T(2,128)} %copy-done.19) | copy-start | bytes 3508
  794.3 257.6 %copy-start.12 = (f32[146,2]{1,0:T(8,128)S(1)}, f32[146,2]{1,0:T(8,128)}, u32[]{:S(2)}) copy-start(f32[146,2]{1,0:T(8,128)} %copy-done.11) | copy-start | bytes 3508
  796.3 259.8 %copy-start.4 = (f32[146,2,1024]{2,1,0:T(2,128)S(1)}, f32[146,2,1024]{2,1,0:T(2,128)}, u32[]{:S(2)}) copy-start(f32[146,2,1024]{2,1,0:T(2,128)} %copy-done.3) | copy-start | bytes 3588100
  1056.1 6.4 copy-start.21
  1061.5 69.4 %reduce-scatter.21.cloned.1.call-start = ((), (), s32[]{:S(2)}) async-start(), calls=%async_computation.16 | async-start | bytes 294912
Sparse Core Ops, SparseCore 0:
  10.5 28.5 all-gather.9
  41.1 50.5 all-gather.7
  119.5 172.7 all-reduce.10
  294.1 26.7 all-gather.13
  322.8 50.5 all-gather.11
  374.9 49.2 all-gather.17
  426.0 26.7 all-gather.15
  471.2 174.0 all-reduce.12
  655.6 49.5 all-gather.19
  708.3 39.7 reduce-scatter.24
  751.4 41.0 reduce-scatter.16
  795.5 34.1 reduce-scatter.22
  832.9 38.3 reduce-scatter.14
  873.6 174.0 all-reduce.14
  1061.7 32.6 reduce-scatter.18
  1097.2 33.7 reduce-scatter.20
where the time goes:
time: 1160 us; the launch traced here: 1150 us
  waiting for transfers between devices  872 us (75%)
  matrix products  77.8 us (7%)
  other arithmetic  64.8 us (6%)
  blocking collectives  55.7 us (5%)
  local copies, waits for them, and re-layouts  51.4 us (4%)
  between operations  15.4 us (1%)
  starting transfers between devices  14.1 us (1%)
    unnamed x23, waiting for transfers between devices  593 us
    all_gather x1, waiting for transfers between devices, body(): gathered2 = lax.all_gather(normed2, 'tensor', axis=0, tiled=True)  52.6 us
    all_gather x1, waiting for transfers between devices, body(): gathered1 = lax.all_gather(normed1, 'tensor', axis=0, tiled=True)  45.4 us
    reduce_scatter x1, waiting for transfers between devices, body(): lax.psum_scatter(grad_w_qkv.astype(jnp.bfloat16), 'dp', scatter_dimension...  40 us
    all_gather x1, waiting for transfers between devices, body(): grad_attn_all = lax.all_gather(grad_attn_low, 'tensor', axis=0, tiled=True)  31.5 us
    all_gather x1, waiting for transfers between devices, body(): grad_gathered = lax.all_gather(cotangent, 'tensor', axis=0, tiled=True)  29.9 us
    all_gather x1, waiting for transfers between devices, gather_layer(): lax.all_gather(w_2, 'dp', axis=1, tiled=True)  28.7 us
    reduce_scatter x1, waiting for transfers between devices, body(): lax.psum_scatter(grad_w_1.astype(jnp.bfloat16), 'dp', scatter_dimension=0...  27.9 us
  transfers between devices with their start and end apart: 16, of which 14 were waited for; matrix products, arithmetic and copies ran while one was open for 10% of the time, Pallas kernels for 0%

commit v1 on v0

--- a/solution.py
+++ b/solution.py
@@ -112,7 +112,27 @@
     )
     hidden1 = residual + attn_sum + shifts[2]
     normed2 = layer_norm(hidden1, gains[1], shifts[1]).astype(jnp.bfloat16)
-    gathered2 = lax.all_gather(normed2, "tensor", axis=0, tiled=True)
+    f_next = lax.psum(1, "tensor")
+    oldest, current_arr, outcome_arr = (f_next, lax.axis_index("tensor"), normed2.shape[0])
+    pool = [ix * oldest if dd == 0 else ix for dd, ix in enumerate(normed2.shape)]
+    gathered2 = lax.dynamic_update_slice_in_dim(
+        jnp.zeros(pool, normed2.dtype), normed2, current_arr * outcome_arr, axis=0
+    )
+    carry_out = carry_in = normed2
+    for hop_no in range(1, oldest // 2 + 1):
+        carry_out = lax.ppermute(
+            carry_out, "tensor", [(dd, (dd + 1) % oldest) for dd in range(oldest)]
+        )
+        gathered2 = lax.dynamic_update_slice_in_dim(
+            gathered2, carry_out, (current_arr - hop_no) % oldest * outcome_arr, axis=0
+        )
+        if 2 * hop_no < oldest:
+            carry_in = lax.ppermute(
+                carry_in, "tensor", [(dd, (dd - 1) % oldest) for dd in range(oldest)]
+            )
+            gathered2 = lax.dynamic_update_slice_in_dim(
+                gathered2, carry_in, (current_arr + hop_no) % oldest * outcome_arr, axis=0
+            )
     hidden_in = jnp.dot(gathered2, wide_up, preferred_element_type=jnp.float32) + b_1.astype(
         jnp.float32
     )

time: 1160 us -> 1110 us (0.957)
  waiting for transfers between devices: 872 us -> 807 us
  local copies, waits for them, and re-layouts: 51.4 us -> 80.9 us
    all_gather x1 -> x0, waiting for transfers between devices: 52.6 us -> none  [body(): gathered2 = lax.all_gather(normed2, 'tensor', axis=0, tiled=True)]
    all_gather x1, waiting for transfers between devices: 29.9 us -> 4.72 us  [body(): grad_gathered = lax.all_gather(cotangent, 'tensor', axis=0, tiled=True)]
    ppermute x0 -> x3, waiting for transfers between devices: none -> 24.2 us  [the longest x2 24.2 us: body(): lax.ppermute(carry_out, 'tensor', [(dd, (dd + 1) % oldest) for dd in rang...]
    all_gather x1, waiting for transfers between devices: 22 us -> 0.01 us  [gather_layer(): lax.all_gather(w_1, 'dp', axis=0, tiled=True)]
    dynamic_update_slice x0 -> x4, local copies, waits for them, and re-layouts: none -> 18.2 us  [the longest x2 9.09 us: body(): lax.dynamic_update_slice_in_dim(gathered2, carry_out, (current_arr - hop_...]
    all_gather x1 -> x0, starting transfers between devices: 13.1 us -> none  [body(): gathered2 = lax.all_gather(normed2, 'tensor', axis=0, tiled=True)]
    unnamed x23 -> x22, waiting for transfers between devices: 593 us -> 605 us
  transfers between devices with their start and end apart: 16 -> 18, of which waited for: 14 -> 14; matrix products, arithmetic and copies ran while one was open for 10% -> 13% of each run, Pallas kernels for 0% -> 0%
where the time goes in v1:
time: 1110 us
  waiting for transfers between devices  807 us (73%)
  local copies, waits for them, and re-layouts  80.9 us (7%)
  matrix products  77.3 us (7%)
  other arithmetic  63.8 us (6%)
  blocking collectives  55.5 us (5%)
  between operations  15.4 us (1%)
    unnamed x22, waiting for transfers between devices  605 us
    all_gather x1, waiting for transfers between devices, body(): gathered1 = lax.all_gather(normed1, 'tensor', axis=0, tiled=True)  46.5 us
    reduce_scatter x1, waiting for transfers between devices, body(): lax.psum_scatter(grad_w_qkv.astype(jnp.bfloat16), 'dp', scatter_dimension...  39.9 us
    all_gather x1, waiting for transfers between devices, body(): grad_attn_all = lax.all_gather(grad_attn_low, 'tensor', axis=0, tiled=True)  32 us
    all_gather x1, waiting for transfers between devices, gather_layer(): lax.all_gather(w_2, 'dp', axis=1, tiled=True)  28.1 us
    reduce_scatter x1, waiting for transfers between devices, body(): lax.psum_scatter(grad_w_1.astype(jnp.bfloat16), 'dp', scatter_dimension=0...  26.2 us
    ppermute x2, waiting for transfers between devices, body(): lax.ppermute(carry_out, 'tensor', [(dd, (dd + 1) % oldest) for dd in rang...  24.2 us
  transfers between devices with their start and end apart: 18, of which 14 were waited for; matrix products, arithmetic and copies ran while one was open for 13% of the time, Pallas kernels for 0%

profile of v1, /device:TPU:0, one launch (start us, length us, event | category | flops | bytes accessed | tf_op | source)
XLA Modules:
  0.0 1105.3 jit_solution(5902295515963264787)
XLA Ops:
  10.8 2.0 fusion.78
  13.0 10.4 all_gather.31
  23.4 8.8 all_gather.32
  34.8 10.4 all_gather.35
  45.3 46.5 %all-gather.7.cloned.1.call-done = bf16[584,2,1024]{2,1,0:T(2,128)(2,1)} async-done(((bf16[146,2,1024]{2,1,0:T(2,128)(2,1)}), bf16[584,2,1024]{2,1,0:T(2,128)(2,1)}) %all-gather.7.cloned.1.call-update) | async-done | bytes 2392080 | tf_op jit(solution)/shard_map/all_gather | solution.py:92
  91.8 5.7 fusion.56
  97.5 2.8 copy.125
  100.2 11.2 %while.22 = (s32[]{:T(128)}, bf16[2,584,4,64]{1,3,2,0:T(8,128)(2,1)}, f32[2,4,584]{2,1,0:T(4,128)S(1)}, bf16[2,584,3,4,64]{1,4,3,2,0:T(8,128)(2,1)S(1)}, s32[2,584]{1,0:T(2,128)S(1)}, /*index=5*/s32[]{:T(128)}) while((s32[]{:T(128)}, bf16[2,584,4,64]{1,3,2,0:T(8,128)(2,1)}, f32[2,4,584]{2,1,0:T(4,128)S(1)}, ...), condition=%wide.region_5.6_spmd, body=%wide.region_2.5_spmd.sunk | while | flops 365759776 | bytes 24867780 | solution.py:104
  111.5 2.0 fusion.87
  113.5 5.9 copy.127
  122.4 170.0 %all-reduce.11.cloned.1.call-done = f32[584,2,1024]{2,1,0:T(2,128)} async-done(((f32[584,2,1024]{2,1,0:T(2,128)}), f32[584,2,1024]{2,1,0:T(2,128)}) %all-reduce.11.cloned.1.call-update) | async-done | bytes 4784144
  292.4 2.3 fusion.97
  297.4 3.8 collective-permute-start.1
  301.2 14.7 %collective-permute-done = bf16[146,2,1024]{2,1,0:T(2,128)(2,1)} collective-permute-done((bf16[146,2,1024]{2,1,0:T(2,128)(2,1)}, bf16[146,2,1024]{2,1,0:T(2,128)(2,1)}, u32[]{:S(2)}, u32[]{:S(2)}) %collective-permute-start) | collective-permute-done | bytes 598048 | tf_op jit(solution)/shard_map/ppermute | solution.py:123
  316.1 2.0 copy.132
  319.8 4.6 dynamic_update_slice.24
  324.4 2.0 copy.133
  326.4 4.5 dynamic_update_slice.25
  331.0 2.1 copy.134
  333.0 4.6 dynamic_update_slice.26
  337.6 9.5 collective-permute-done.2
  347.1 2.0 copy.135
  349.2 4.6 dynamic_update_slice.27
  353.8 6.5 fusion.85
  360.3 2.2 copy-done.9
  362.4 12.2 %multiply_convert_fusion.1 = (bf16[584,2,1024]{2,0,1:T(8,128)(2,1)}, f32[584,2,1024]{2,0,1:T(8,128)}) fusion(f32[584,2,1024]{2,0,1:T(8,128)S(1)} %get-tuple-element.161, f32[1024]{0:T(1024)S(1)} %convert_element_type.124, u8[584,1024]{1,0:T(8,128)(4,1)S(1)} %get-tuple-element.107, u8[584,1024]{1,0:T(8,128)(4,1)S(1)} %get-tuple-element.106), kind=kLoop, calls=%fused_computation.55 | loop fusion | flops 84918272 | bytes 13160448 | tf_op jit(solution)/shard_map/convert_element_type | solution.py:139
  374.7 4.7 all-gather.15.cloned.1.call-done
  379.4 28.1 %all-gather.13.cloned.1.call-done = bf16[1024,1024]{1,0:T(8,128)(2,1)} async-done(((bf16[1024,128]{1,0:T(8,128)(2,1)}), bf16[1024,1024]{1,0:T(8,128)(2,1)}) %all-gather.13.cloned.1.call-update) | async-done | bytes 2097168 | tf_op jit(solution)/shard_map/all_gather | solution.py:29
  407.5 9.5 fusion.102
  417.0 2.7 fusion.49
  419.8 5.9 copy.138
  425.7 174.2 %all-reduce.13.cloned.1.call-done = f32[584,2,1024]{2,1,0:T(2,128)} async-done(((f32[584,2,1024]{2,1,0:T(2,128)}), f32[584,2,1024]{2,1,0:T(2,128)}) %all-reduce.13.cloned.1.call-update) | async-done | bytes 4784144
  599.9 3.7 multiply_reduce_fusion.1
  603.8 3.1 fusion.96
  609.9 6.8 bitcast_convert_fusion
  616.7 4.0 copy.178
  620.7 6.7 bitcast_convert_fusion.1
  627.5 32.0 %all-gather.17.cloned.1.call-done = bf16[584,2,1024]{2,1,0:T(2,128)(2,1)} async-done(((bf16[146,2,1024]{2,1,0:T(2,128)(2,1)}), bf16[584,2,1024]{2,1,0:T(2,128)(2,1)}) %all-gather.17.cloned.1.call-update) | async-done | bytes 2392080 | tf_op jit(solution)/shard_map/all_gather | solution.py:176
  659.5 3.7 fusion.70
  663.2 2.1 copy.176
  665.3 3.6 fusion.67
  668.9 2.2 copy.144
  671.1 23.7 %while.23 = (s32[]{:T(128)}, f32[2,584,3,4,64]{1,4,3,2,0:T(8,128)}, bf16[2,584,3,4,64]{1,4,3,2,0:T(8,128)(2,1)S(1)}, s32[2,584]{1,0:T(2,128)S(1)}, f32[2,4,584]{...) while((s32[]{:T(128)}, f32[2,584,3,4,64]{1,4,3,2,0:T(8,128)}, ...), condition=%wide.region_15.16_spmd, body=%wide.region_13.15_spmd.sunk | while | flops 894760960 | bytes 83480296 | solution.py:186
  674.3 2.0 multiply_reduce_fusion.5
  685.9 2.0 multiply_reduce_fusion.5
  694.9 2.7 bitcast_convert_fusion.2
  697.9 4.0 bitcast_convert_fusion.3
  702.1 5.0 fusion.53
  707.1 4.0 copy.136
  711.1 2.1 convolution_convert_fusion
  713.1 4.0 copy.147
  720.8 26.2 %reduce-scatter.17.cloned.1.call-done = bf16[128,1024]{1,0:T(8,128)(2,1)} async-done(((bf16[1024,1024]{1,0:T(8,128)(2,1)}), bf16[128,1024]{1,0:T(8,128)(2,1)}) %reduce-scatter.17.cloned.1.call-update) | async-done | bytes 262160 | tf_op jit(solution)/shard_map/reduce_scatter | solution.py:236
  748.8 1.9 slice_reduce_fusion.1
  750.8 13.7 %all-reduce.4 = (f32[2,256]{1,0:T(2,128)}, f32[1024]{0:T(1024)}) all-reduce(f32[2,256]{1,0:T(2,128)S(1)} %pad_maximum_fusion.2, f32[1024]{0:T(1024)S(1)} %get-tuple-element.162), channel_id=1, replica_groups=mesh['dp'=8,'tensor'=4] {'dp'}, use_global_device_ids=true, to_apply=%region_32.33 | all-reduce | flops 1536 | bytes 12288 | tf_op jit(solution)/shard_map/psum | solution.py:244
  764.5 19.7 %reduce-scatter.23.cloned.1.call-done = bf16[128,256]{1,0:T(8,128)(2,1)} async-done(((bf16[1024,256]{1,0:T(8,128)(2,1)}), bf16[128,256]{1,0:T(8,128)(2,1)}) %reduce-scatter.23.cloned.1.call-update) | async-done | bytes 65552
  785.8 39.9 %reduce-scatter.15.cloned.1.call-done = bf16[128,3,256]{2,0,1:T(8,128)(2,1)} async-done(((bf16[1024,3,256]{2,0,1:T(8,128)(2,1)}), bf16[128,3,256]{2,0,1:T(8,128)(2,1)}) %reduce-scatter.15.cloned.1.call-update) | async-done | bytes 196624 | tf_op jit(solution)/shard_map/reduce_scatter | solution.py:230
  827.4 174.8 %all-reduce.15.cloned.1.call-done = (bf16[584,2,1024]{2,1,0:T(2,128)(2,1)}, bf16[584,2,1024]{2,1,0:T(2,128)(2,1)}) async-done(((bf16[584,2,1024]{2,1,0:T(2,128)(2,1)}, bf16[584,2,1024]{2,1,0:T(2,128)(2,1)}), (bf16[584,2,1024]{2,1,0:T(2,128)(2,1)}, bf16[584,2,1024]{2,1,0:T(2,128)(2,1)})) %all-reduce.15.cloned.1.call-update) | async-done | bytes 4784144
  1003.9 2.3 fusion.83
  1006.4 4.2 fusion.79
  1010.7 4.5 add_add_fusion.2
  1017.1 2.5 add_convert_fusion.1
  1019.6 29.3 %reduce-scatter.19.cloned.1.call-done = bf16[128,2]{1,0:T(8,128)(2,1)} async-done(((bf16[1024,2]{1,0:T(8,128)(2,1)}), bf16[128,2]{1,0:T(8,128)(2,1)}) %reduce-scatter.19.cloned.1.call-update) | async-done | bytes 528
  1049.7 35.8 %reduce-scatter.21.cloned.1.call-done = bf16[128,4]{1,0:T(8,128)(2,1)} async-done(((bf16[1024,4]{1,0:T(8,128)(2,1)}), bf16[128,4]{1,0:T(8,128)(2,1)}) %reduce-scatter.21.cloned.1.call-update) | async-done | bytes 1040
  1086.3 12.3 %all-reduce.5 = (f32[2,128]{1,0:T(2,128)}, f32[4,128]{1,0:T(4,128)}) all-reduce(bf16[2,128]{1,0:T(2,128)(2,1)S(1)} %copy.173, bf16[4,128]{1,0:T(4,128)(2,1)S(1)} %copy.175), channel_id=1, replica_groups=mesh['dp'=8,'tensor'=4] {'tensor'}, use_global_device_ids=true, to_apply=%region_22.23 | all-reduce | flops 768 | bytes 4608 | tf_op jit(solution)/shard_map/psum | solution.py:243
  (189 shorter events, 61.4 us)
Async XLA Ops:
  7.2 25.6 %copy-start = (bf16[146,2,1024]{2,1,0:T(2,128)(2,1)S(1)}, bf16[146,2,1024]{2,1,0:T(2,128)(2,1)}, u32[]{:S(2)}) copy-start(bf16[146,2,1024]{2,1,0:T(2,128)(2,1)} %param.15) | copy-start | bytes 1794052
  7.2 27.6 %copy-start.19 = (bf16[256,128]{1,0:T(8,128)(2,1)S(1)}, bf16[256,128]{1,0:T(8,128)(2,1)}, u32[]{:S(2)}) copy-start(bf16[256,128]{1,0:T(8,128)(2,1)} %param.22) | copy-start | bytes 196612
  7.2 38.0 %copy-start.23 = (bf16[2,256]{1,0:T(2,128)(2,1)S(1)}, bf16[2,256]{1,0:T(2,128)(2,1)}, u32[]{:S(2)}) copy-start(bf16[2,256]{1,0:T(2,128)(2,1)} %param.21) | copy-start | bytes 3076
  7.2 38.1 %all-gather.9.cloned.1.call-start = ((), (), s32[]{:S(2)}) async-start(), calls=%async_computation.7 | async-start | bytes 1769472 | tf_op jit(solution)/shard_map/all_gather | solution.py:26
  9.1 82.7 %all-gather.7.cloned.1.call-start = ((), (), s32[]{:S(2)}) async-start(), calls=%async_computation.6 | async-start | bytes 2990080 | tf_op jit(solution)/shard_map/all_gather | solution.py:92
  10.7 86.7 %copy-start.10 = (f32[146,2]{1,0:T(8,128)}, f32[146,2]{1,0:T(8,128)S(1)}, u32[]{:S(2)}) copy-start(f32[146,2]{1,0:T(8,128)S(1)} %broadcast_multiply_fusion.1) | copy-start | bytes 3508
  12.9 10.5 copy-start.20
  13.0 84.4 %copy-start.12 = (f32[146,2]{1,0:T(8,128)}, f32[146,2]{1,0:T(8,128)S(1)}, u32[]{:S(2)}) copy-start(f32[146,2]{1,0:T(8,128)S(1)} %copy.122) | copy-start | bytes 3508
  32.2 65.2 %copy-start.17 = (f32[1,1024]{1,0:T(1,128)}, f32[1,1024]{1,0:T(1,128)S(1)}, u32[]{:S(2)}) copy-start(f32[1,1024]{1,0:T(1,128)S(1)} %get-tuple-element.158) | copy-start | bytes 12292
  34.7 257.7 %all-reduce.11.cloned.1.call-start = ((), (), s32[]{:S(2)}) async-start(), calls=%async_computation.18 | async-start | bytes 9568256
  97.4 2.8 copy-start.16
  101.8 1.4 copy-start.14
  105.0 0.9 copy-start.15
  107.4 1.4 copy-start.14
  110.6 0.9 copy-start.15
  119.4 1.8 copy-start.28
  119.4 234.4 %all-gather.11.cloned.1.call-start = ((), (), s32[]{:S(2)}) async-start(), calls=%async_computation.8 | async-start | bytes 2359296 | tf_op jit(solution)/shard_map/all_gather | solution.py:28
  120.0 259.4 %all-gather.15.cloned.1.call-start = ((), (), s32[]{:S(2)}) async-start(), calls=%async_computation.10 | async-start | bytes 2990080 | tf_op jit(solution)/shard_map/all_gather | solution.py:154
  120.6 286.9 %all-gather.13.cloned.1.call-start = ((), (), s32[]{:S(2)}) async-start(), calls=%async_computation.9 | async-start | bytes 2359296 | tf_op jit(solution)/shard_map/all_gather | solution.py:29
  294.7 21.4 %copy-start.24 = (bf16[1024]{0:T(1024)(128)(2,1)S(1)}, bf16[1024]{0:T(1024)(128)(2,1)}, u32[]{:S(2)}) copy-start(bf16[1024]{0:T(1024)(128)(2,1)} %param.24) | copy-start | bytes 6148
  297.4 18.5 %collective-permute-start = (bf16[146,2,1024]{2,1,0:T(2,128)(2,1)}, bf16[146,2,1024]{2,1,0:T(2,128)(2,1)}, u32[]{:S(2)}, u32[]{:S(2)}) collective-permute-start(bf16[146,2,1024]{2,1,0:T(2,128)(2,1)} %add_convert_fusion.2), channel_id=1, source_target_pairs={{0,1},{1,2},{2,3},{3,0},{4,5},{5,6},{6,7},{7,4},{8,9},{9,10},{10,1... | collective-permute-start | bytes 1794056 | tf_op jit(solution)/shard_map/ppermute | solution.py:123
  297.4 33.5 %collective-permute-start.1 = (bf16[146,2,1024]{2,1,0:T(2,128)(2,1)}, bf16[146,2,1024]{2,1,0:T(2,128)(2,1)}, u32[]{:S(2)}, u32[]{:S(2)}) collective-permute-start(bf16[146,2,1024]{2,1,0:T(2,128)(2,1)} %add_convert_fusion.2), channel_id=1, source_target_pairs={{0,3},{1,0},{2,1},{3,2},{4,7},{5,4},{6,5},{7,6},{8,11},{9,8},{10,9... | collective-permute-start | bytes 1794056 | tf_op jit(solution)/shard_map/ppermute | solution.py:130
  315.9 31.2 %collective-permute-start.2 = (bf16[146,2,1024]{2,1,0:T(2,128)(2,1)}, bf16[146,2,1024]{2,1,0:T(2,128)(2,1)}, u32[]{:S(2)}, u32[]{:S(2)}) collective-permute-start(bf16[146,2,1024]{2,1,0:T(2,128)(2,1)} %collective-permute-done), channel_id=1, source_target_pairs={{0,1},{1,2},{2,3},{3,0},{4,5},{5,6},{6,7},{7,4},{8,9},{9,10},{10,1... | collective-permute-start | bytes 1794056 | tf_op jit(solution)/shard_map/ppermute | solution.py:123
  315.9 284.0 %all-reduce.13.cloned.1.call-start = ((), (), s32[]{:S(2)}) async-start(), calls=%async_computation.19 | async-start | bytes 9568256
  360.2 2.2 copy-start.9
  407.5 9.6 copy-start.26
  417.0 2.7 copy-start.29
  425.7 233.9 %all-gather.17.cloned.1.call-start = ((), (), s32[]{:S(2)}) async-start(), calls=%async_computation.11 | async-start | bytes 2990080 | tf_op jit(solution)/shard_map/all_gather | solution.py:176
  603.8 4.2 copy-start.6
  607.0 1.0 copy-start.4
  609.9 108.9 %reduce-scatter.25.cloned.1.call-start = ((), (), s32[]{:S(2)}) async-start(), calls=%async_computation.17 | async-start | bytes 2359296
  620.7 126.3 %reduce-scatter.17.cloned.1.call-start = ((), (), s32[]{:S(2)}) async-start(), calls=%async_computation.13 | async-start | bytes 2359296 | tf_op jit(solution)/shard_map/reduce_scatter | solution.py:236
  627.5 156.7 %reduce-scatter.23.cloned.1.call-start = ((), (), s32[]{:S(2)}) async-start(), calls=%async_computation.16 | async-start | bytes 589824
  671.6 1.2 copy-start.8
  678.9 2.1 copy-start.2
  681.2 1.9 copy-start.3
  683.3 1.2 copy-start.8
  690.5 2.2 copy-start.2
  692.9 1.9 copy-start.3
  694.8 130.9 %reduce-scatter.15.cloned.1.call-start = ((), (), s32[]{:S(2)}) async-start(), calls=%async_computation.12 | async-start | bytes 1769472 | tf_op jit(solution)/shard_map/reduce_scatter | solution.py:230
  694.8 3.0 copy-start.25
  701.9 300.4 %all-reduce.15.cloned.1.call-start = ((), (), s32[]{:S(2)}) async-start(), calls=%async_computation.20 | async-start | bytes 9568256
  707.1 4.0 copy-start.27
  717.1 1.1 copy-start.7
  717.2 331.7 %reduce-scatter.19.cloned.1.call-start = ((), (), s32[]{:S(2)}) async-start(), calls=%async_computation.14 | async-start | bytes 294912
  720.8 283.1 %copy-start.1 = (bf16[146,2,1024]{2,1,0:T(2,128)(2,1)S(1)}, bf16[146,2,1024]{2,1,0:T(2,128)(2,1)}, u32[]{:S(2)}) copy-start(bf16[146,2,1024]{2,1,0:T(2,128)(2,1)} %param.15) | copy-start | bytes 1794052
  720.8 283.1 %copy-start.11 = (f32[146,2]{1,0:T(8,128)S(1)}, f32[146,2]{1,0:T(8,128)}, u32[]{:S(2)}) copy-start(f32[146,2]{1,0:T(8,128)} %copy-done.10) | copy-start | bytes 3508
  720.8 283.1 %copy-start.18 = (f32[1,1024]{1,0:T(1,128)S(1)}, f32[1,1024]{1,0:T(1,128)}, u32[]{:S(2)}) copy-start(f32[1,1024]{1,0:T(1,128)} %copy-done.17) | copy-start | bytes 12292
  748.8 257.5 %copy-start.21 = (f32[146,2]{0,1:T(2,128)S(1)}, f32[146,2]{0,1:T(2,128)}, u32[]{:S(2)}) copy-start(f32[146,2]{0,1:T(2,128)} %copy-done.20) | copy-start | bytes 3508
  748.8 257.6 %copy-start.13 = (f32[146,2]{1,0:T(8,128)S(1)}, f32[146,2]{1,0:T(8,128)}, u32[]{:S(2)}) copy-start(f32[146,2]{1,0:T(8,128)} %copy-done.12) | copy-start | bytes 3508
  750.8 259.9 %copy-start.5 = (f32[146,2,1024]{2,1,0:T(2,128)S(1)}, f32[146,2,1024]{2,1,0:T(2,128)}, u32[]{:S(2)}) copy-start(f32[146,2,1024]{2,1,0:T(2,128)} %copy-done.4) | copy-start | bytes 3588100
  1010.7 6.4 copy-start.22
  1016.1 69.4 %reduce-scatter.21.cloned.1.call-start = ((), (), s32[]{:S(2)}) async-start(), calls=%async_computation.15 | async-start | bytes 294912
Sparse Core Ops, SparseCore 0:
  10.5 28.4 all-gather.8
  41.1 50.5 all-gather.6
  119.5 172.7 all-reduce.10
  294.1 26.7 all-gather.10
  322.3 57.0 all-gather.14
  381.1 26.2 all-gather.12
  425.8 174.0 all-reduce.12
  610.0 49.5 all-gather.16
  662.8 39.7 reduce-scatter.24
  705.8 41.1 reduce-scatter.16
  750.0 34.0 reduce-scatter.22
  787.3 38.3 reduce-scatter.14
  828.1 174.0 all-reduce.14
  1016.2 32.6 reduce-scatter.18
  1051.7 33.7 reduce-scatter.20
